TPU v7x, 32 devices: a whole 2x2x4 slice. The times are simulated.
32 devices in a mesh: row: 4 (over x, core), col: 8 (over z, y).
Axes of the slice: x: 2, y: 2, z: 4, core: 2. Of those that a mesh axis runs over, the one named last changes fastest.
Arguments:
- hamiltonian: bfloat16 [2912, 2912], P('row', 'col'), may hold values from -6 to 6
- new_atom: int32 [224], replicated, may hold values from 0 to 223, as said below
- pattern: int32 [224, 224], P('row', 'col'), may hold values 0 or 1
Outputs:
- sign_matrix: float32 [2912, 2912], P('row', 'col')
Inputs may be any that keep to these rules, and one draw needn't show every extreme that they name: `new_atom`: each old atom appears once. Block column b holds atoms b * 28 to (b + 1) * 28 - 1 in both orders. For each new block column d and each v from 0 to 27, exactly one atom of new block column d comes from old block column (d - 1 - (v mod 8)) mod 8, so the number of atoms that old block column b sends to new block column (b + k) mod 8 is the number of such v with (1 + v) mod 8 = k.
All inputs are finite; a program needn't handle non-finite values. No bound on the sum of `pattern` on one device may be relied on, other than what follows from the above.
Results may differ from a plain program's by a relative error of at most 0.0029.
Values may be sent and summed in bfloat16 or wider, within the bound.
A program may use at most 64 MiB of HBM per device.

v0:
```python
import jax
import jax.numpy as jnp
from jax import lax
from jax.sharding import PartitionSpec as P

NBF = 13
BF = jnp.bfloat16
F32 = jnp.float32


def mm(a, b):
    return jnp.dot(a, b, preferred_element_type=F32)


def spread(n):
    i = lax.broadcasted_iota(jnp.int32, (n * NBF, n), 0)
    a = lax.broadcasted_iota(jnp.int32, (n * NBF, n), 1) * NBF
    return (i >= a) & (i < a + NBF)


def on_device(hamiltonian, new_atom, pattern):
    rows_here, cols_here = hamiltonian.shape
    order = rows_here * lax.axis_size("row")
    atoms = order // NBF
    ar, ac = pattern.shape
    row_here = lax.axis_index("row")
    col_here = lax.axis_index("col")
    panel = lax.all_gather(hamiltonian, "col", axis=1, tiled=True)
    pat = lax.all_gather(pattern.astype(BF), ("row", "col"), axis=0, tiled=False)
    n_row, n_col = (lax.axis_size("row"), lax.axis_size("col"))
    pat = pat.reshape(n_row, n_col, ar, ac).transpose(0, 2, 1, 3).reshape(atoms, atoms)
    old = jnp.arange(atoms, dtype=jnp.int32)
    perm = (new_atom[:, None] == old[None, :]).astype(BF)
    mine = (new_atom[None, :] == row_here * ar + jnp.arange(ar, dtype=jnp.int32)[:, None]).astype(
        BF
    )
    pat_rows = mm(mine, pat).astype(BF)
    e_row = spread(ar)
    e_col = spread(ac)
    e_rowb = e_row.astype(BF)
    rows_masked = mm(e_rowb, mm(pat_rows, perm).astype(BF)).astype(BF)
    keep = mm(rows_masked, spread(atoms).astype(BF).T).astype(BF)
    m = panel * keep
    total = lax.psum(jnp.sum(m.astype(F32) ** 2), "row")
    s = lax.rsqrt(total / order)

    def old_index(n, here, e):
        mine_atoms = lax.dynamic_slice_in_dim(new_atom, here * n, n)
        base = jnp.sum(
            jnp.where(e, (mine_atoms - jnp.arange(n, dtype=jnp.int32))[None, :], 0), axis=1
        )
        return base * NBF + jnp.arange(n * NBF, dtype=jnp.int32)

    full = jnp.arange(order, dtype=jnp.int32)
    pick_col = (full[:, None] == old_index(ac, col_here, e_col)[None, :]).astype(BF)
    pick_row = (old_index(ar, row_here, e_row)[:, None] == full[None, :]).astype(BF)
    right = lax.all_gather(mm(m, pick_col).astype(BF), "row", axis=0, tiled=True)
    e_colt = e_col.astype(BF).T
    here_cols = lax.dynamic_slice_in_dim(pat_rows, col_here * ac, ac, axis=1)
    keep_sq = mm(mm(e_rowb, here_cols).astype(BF), e_colt)
    square = (mm(m, right) * (s * s) * keep_sq).astype(BF)
    square = lax.all_gather(square, "row", axis=0, tiled=True)
    cube = lax.all_gather((mm(m, square) * s).astype(BF), "row", axis=0, tiled=True)
    start = (mm(pick_row, right) * s).astype(BF).astype(F32)
    keep_out = mm(mm(e_rowb, pattern.astype(BF)).astype(BF), e_colt)
    return keep_out * (1.5 * start - 0.5 * mm(pick_row, cube))


def solution(mesh):
    in_specs = (P("row", "col"), P(), P("row", "col"))
    out_specs = P("row", "col")
    return jax.shard_map(
        on_device, mesh=mesh, in_specs=in_specs, out_specs=out_specs, check_vma=False
    )
```

profile of v0, /device:TPU:0, one launch (start us, length us, event | category | flops | bytes accessed | tf_op | source)
XLA Modules:
  0.0 211.8 jit_solution(7994260219636314159)
XLA Ops:
  6.5 0.0 all-gather.14.cloned.1.call-start
  6.5 0.7 all-gather.14.cloned.1.call-update
  7.3 0.0 all-gather.8.cloned.1.call-start
  7.3 0.7 convert_bitcast_fusion
  8.0 75.1 %all-gather.2 = bf16[32,56,28]{1,2,0:T(8,128)(2,1)S(1)} all-gather(bf16[1,56,28]{1,2,0:T(8,128)(2,1)S(1)} %convert_bitcast_fusion), channel_id=2, replica_groups=mesh['row'=4,'col'=8] {'row','col'}, dimensions={0}, use_global_device_ids=true | all-gather | bytes 103488 | tf_op jit(solution)/shard_map/all_gather | solution.py:29
  83.2 0.2 copy.12
  83.3 0.2 reshape.30
  83.5 0.8 iota_subtract_fusion
  84.3 0.1 select_reduce_fusion.1
  84.4 0.9 convolution_convert_fusion.5
  85.3 0.9 convolution_convert_fusion.4
  86.2 5.0 %all-gather.14.cloned.1.call-done = bf16[8,364,728]{1,2,0:T(8,128)(2,1)} async-done(((bf16[1,364,728]{1,2,0:T(8,128)(2,1)}), bf16[8,364,728]{1,2,0:T(8,128)(2,1)}) %all-gather.14.cloned.1.call-update) | async-done | bytes 4239888 | tf_op jit(solution)/shard_map/all_gather | solution.py:28
  91.2 4.9 %copy.9 = bf16[8,364,728]{1,0,2:T(8,128)(2,1)} copy(bf16[8,364,728]{1,2,0:T(8,128)(2,1)} %all-gather.14.cloned.1.call-done) | data formatting | bytes 8479744 | tf_op jit(solution)/shard_map/all_gather | solution.py:28
  96.1 8.6 %reshape.34 = bf16[2912,728]{0,1:T(8,128)(2,1)} reshape(bf16[8,364,728]{1,0,2:T(8,128)(2,1)} %copy.9) | data formatting | bytes 8479744
  104.7 6.9 %multiply_reduce_fusion = (f32[]{:T(128)}, bf16[728,2912]{1,0:T(8,128)(2,1)}) fusion(s32[224]{0:T(256)S(1)} %get-tuple-element.8, s32[224]{0:T(256)S(1)} %get-tuple-element.7, bf16[56,224]{1,0:T(8,128)(2,1)S(1)} %convolution_convert_fusion.4, s32[56]{0:T(128)S(1)} %get-tuple-element.10, s32[56]{0:T(128)S(1)} %get-tuple-element.9, bf16[2912,728]{0,1:T(8,128)(2,1)} %reshape.34), kind=kOutput, calls=%fused_computation | convolution fusion | flops 987197120 | bytes 8507076 | tf_op jit(solution)/shard_map/dot_general | solution.py:12
  111.6 5.5 %fusion.19 = bf16[728,364]{1,0:T(8,128)(2,1)} fusion(bf16[728,2912]{1,0:T(8,128)(2,1)} %get-tuple-element.6, s32[364]{0:T(512)S(1)} %iota_add_fusion.1), kind=kOutput, calls=%fused_computation.28 | convolution fusion | flops 1544638336 | bytes 4771312 | tf_op jit(solution)/shard_map/dot_general | solution.py:12
  117.1 0.0 all-gather.8.cloned.1.call-update
  117.1 0.0 all-gather.10.cloned.1.call-start
  117.2 6.2 %psum.7 = f32[]{:T(128)} all-reduce(f32[]{:T(128)} %get-tuple-element.5), channel_id=1, replica_groups=mesh['row'=4,'col'=8] {'row'}, use_global_device_ids=true, to_apply=%region_3.4 | all-reduce | flops 1 | bytes 8 | tf_op jit(solution)/shard_map/psum | solution.py:44
  124.2 15.2 %all-gather.8.cloned.1.call-done = bf16[2912,364]{1,0:T(8,128)(2,1)} async-done(((bf16[728,364]{1,0:T(8,128)(2,1)}), bf16[2912,364]{1,0:T(8,128)(2,1)}) %all-gather.8.cloned.1.call-update) | async-done | bytes 2119952 | tf_op jit(solution)/shard_map/all_gather | solution.py:57
  139.3 5.4 %convolution_multiply_fusion.1 = f32[728,364]{1,0:T(8,128)S(1)} fusion(bf16[728,2912]{1,0:T(8,128)(2,1)} %get-tuple-element.6, bf16[2912,364]{1,0:T(8,128)(2,1)} %all-gather.8.cloned.1.call-done, f32[]{:T(128)S(6)} %mul.104), kind=kOutput, calls=%fused_computation.17 | convolution fusion | flops 1543578368 | bytes 7419780 | tf_op jit(solution)/shard_map/dot_general | solution.py:12
  144.7 1.5 fusion.17
  146.2 0.0 all-gather.10.cloned.1.call-update
  146.2 0.0 copy-start.1
  146.2 0.0 copy-start.2
  146.2 0.2 all-gather.12.cloned.1.call-start
  146.5 23.3 %all-gather.10.cloned.1.call-done = bf16[2912,364]{1,0:T(8,128)(2,1)} async-done(((bf16[728,364]{1,0:T(8,128)(2,1)}), bf16[2912,364]{1,0:T(8,128)(2,1)}) %all-gather.10.cloned.1.call-update) | async-done | bytes 2119952 | tf_op jit(solution)/shard_map/all_gather | solution.py:62
  169.7 6.2 %fusion.18 = bf16[728,364]{1,0:T(8,128)(2,1)} fusion(bf16[728,2912]{1,0:T(8,128)(2,1)} %get-tuple-element.6, bf16[2912,364]{1,0:T(8,128)(2,1)} %all-gather.10.cloned.1.call-done, f32[]{:T(128)S(6)} %rsqrt.3), kind=kOutput, calls=%fused_computation.27 | convolution fusion | flops 1543843328 | bytes 6889796 | tf_op jit(solution)/shard_map/dot_general | solution.py:12
  175.9 0.0 all-gather.12.cloned.1.call-update
  176.0 0.0 copy-done.1
  176.0 0.1 iota_subtract_fusion.1
  176.1 0.1 select_reduce_fusion
  176.2 0.0 copy-done.2
  176.2 2.5 %fusion.16 = f32[728,364]{1,0:T(8,128)S(1)} fusion(bf16[2912,364]{1,0:T(8,128)(2,1)S(1)} %copy-done.2, s32[728]{0:T(1024)S(1)} %iota_add_fusion, f32[]{:T(128)S(6)} %rsqrt.3), kind=kOutput, calls=%fused_computation.25 | convolution fusion | flops 1546493184 | bytes 3182820 | tf_op jit(solution)/shard_map/dot_general | solution.py:12
  178.7 0.0 copy-start
  178.7 20.7 %all-gather.12.cloned.1.call-done = bf16[2912,364]{1,0:T(8,128)(2,1)} async-done(((bf16[728,364]{1,0:T(8,128)(2,1)}), bf16[2912,364]{1,0:T(8,128)(2,1)}) %all-gather.12.cloned.1.call-update) | async-done | bytes 2119952 | tf_op jit(solution)/shard_map/all_gather | solution.py:63
  199.5 4.1 %fusion.13 = f32[728,364]{1,0:T(8,128)S(1)} fusion(f32[728,364]{1,0:T(8,128)S(1)} %fusion.16, bf16[2912,364]{1,0:T(8,128)(2,1)} %all-gather.12.cloned.1.call-done, s32[728]{0:T(1024)S(1)} %iota_add_fusion), kind=kOutput, calls=%fused_computation.22 | convolution fusion | flops 1545963264 | bytes 4242784 | tf_op jit(solution)/shard_map/dot_general | solution.py:12
  203.6 0.0 copy-done
  203.6 1.6 convolution_multiply_fusion.3
  (6 shorter events, 0.0 us)
Async XLA Ops:
  6.5 84.7 %all-gather.14.cloned.1.call-start = ((), (), s32[]{:S(2)}) async-start(), calls=%async_computation.3 | async-start | bytes 5031936 | tf_op jit(solution)/shard_map/all_gather | solution.py:28
  7.3 132.1 %all-gather.8.cloned.1.call-start = ((), (), s32[]{:S(2)}) async-start(), calls=%async_computation | async-start | bytes 2795520 | tf_op jit(solution)/shard_map/all_gather | solution.py:57
  117.1 52.6 %all-gather.10.cloned.1.call-start = ((), (), s32[]{:S(2)}) async-start(), calls=%async_computation.1 | async-start | bytes 2795520 | tf_op jit(solution)/shard_map/all_gather | solution.py:62
  146.2 29.8 %copy-start.1 = (s32[224]{0:T(256)S(1)}, s32[224]{0:T(256)}, u32[]{:S(2)}) copy-start(s32[224]{0:T(256)} %param.4) | copy-start | bytes 2692
  146.2 30.0 %copy-start.2 = (bf16[2912,364]{1,0:T(8,128)(2,1)S(1)}, bf16[2912,364]{1,0:T(8,128)(2,1)}, u32[]{:S(2)}) copy-start(bf16[2912,364]{1,0:T(8,128)(2,1)} %all-gather.8.cloned.1.call-done) | copy-start | bytes 6359812
  146.2 53.2 %all-gather.12.cloned.1.call-start = ((), (), s32[]{:S(2)}) async-start(), calls=%async_computation.2 | async-start | bytes 2795520 | tf_op jit(solution)/shard_map/all_gather | solution.py:63
  178.7 24.9 %copy-start = (s32[56,28]{0,1:T(8,128)S(1)}, s32[56,28]{0,1:T(8,128)}, u32[]{:S(2)}) copy-start(s32[56,28]{0,1:T(8,128)} %param.5) | copy-start | bytes 18820
Sparse Core Ops, SparseCore 0:
  9.5 81.6 all-gather.13
  117.2 22.0 all-gather.7
  146.3 23.3 all-gather.9
  176.1 23.3 all-gather.11
where the time goes:
time: 212 us
  blocking collectives  81.4 us (38%)
  waiting for transfers between devices  64.9 us (31%)
  matrix products  35.5 us (17%)
  between operations  14 us (7%)
  local copies, waits for them, and re-layouts  13.8 us (7%)
    all_gather x1, blocking collectives, on_device(): lax.all_gather(pattern.astype(BF), ('row', 'col'), axis=0, tiled=False)  75.1 us
    dot_general x10, matrix products, mm(): return jnp.dot(a, b, preferred_element_type=F32)  35.5 us
    all_gather x1, waiting for transfers between devices, on_device(): square = lax.all_gather(square, 'row', axis=0, tiled=True)  23.3 us
    all_gather x1, waiting for transfers between devices, on_device(): lax.all_gather((mm(m, square) * s).astype(BF), 'row', axis=0, tiled=True)  20.7 us
    all_gather x1, waiting for transfers between devices, on_device(): lax.all_gather(mm(m, pick_col).astype(BF), 'row', axis=0, tiled=True)  15.2 us
    unnamed x7, local copies, waits for them, and re-layouts  8.62 us
    psum x1, blocking collectives, on_device(): total = lax.psum(jnp.sum(m.astype(F32) ** 2), 'row')  6.25 us
    all_gather x1, waiting for transfers between devices, on_device(): panel = lax.all_gather(hamiltonian, 'col', axis=1, tiled=True)  5 us
  transfers between devices with their start and end apart: 4, of which 4 were waited for; matrix products, arithmetic and copies ran while one was open for 3% of the time, Pallas kernels for 0%

commit v1 on v0

--- a/solution.py
+++ b/solution.py
@@ -59,7 +59,15 @@
     here_cols = lax.dynamic_slice_in_dim(pat_rows, col_here * ac, ac, axis=1)
     keep_sq = mm(mm(e_rowb, here_cols).astype(BF), e_colt)
     square = (mm(m, right) * (s * s) * keep_sq).astype(BF)
-    square = lax.all_gather(square, "row", axis=0, tiled=True)
+    ways, here_2 = (lax.axis_size("row"), lax.axis_index("row"))
+    grown, reach = (square, 1)
+    while reach < ways:
+        theirs = lax.ppermute(grown, "row", [(d, d ^ reach) for d in range(ways)])
+        mine_first = jnp.concatenate([grown, theirs], axis=0)
+        theirs_first = jnp.concatenate([theirs, grown], axis=0)
+        grown = jnp.where(here_2 & reach == 0, mine_first, theirs_first)
+        reach = 2 * reach
+    square = grown
     cube = lax.all_gather((mm(m, square) * s).astype(BF), "row", axis=0, tiled=True)
     start = (mm(pick_row, right) * s).astype(BF).astype(F32)
     keep_out = mm(mm(e_rowb, pattern.astype(BF)).astype(BF), e_colt)

time: 212 us -> 218 us (1.028)
  waiting for transfers between devices: 64.9 us -> 68.9 us
    ppermute x0 -> x2, waiting for transfers between devices: none -> 28.3 us  [on_device(): theirs = lax.ppermute(grown, 'row', [(d, d ^ reach) for d in range(ways)])]
    all_gather x1 -> x0, waiting for transfers between devices: 23.3 us -> none  [on_device(): square = lax.all_gather(square, 'row', axis=0, tiled=True)]
  transfers between devices with their start and end apart: 4 -> 5, of which waited for: 4 -> 5; matrix products, arithmetic and copies ran while one was open for 3% -> 3% of each run, Pallas kernels for 0% -> 0%
where the time goes in v1:
time: 218 us; the launch traced here: 217 us
  blocking collectives  81.5 us (37%)
  waiting for transfers between devices  68.9 us (32%)
  matrix products  36.1 us (17%)
  between operations  13.9 us (6%)
  local copies, waits for them, and re-layouts  13.8 us (6%)
  other arithmetic  2.24 us (1%)
    all_gather x1, blocking collectives, on_device(): lax.all_gather(pattern.astype(BF), ('row', 'col'), axis=0, tiled=False)  75.1 us
    dot_general x10, matrix products, mm(): return jnp.dot(a, b, preferred_element_type=F32)  36.1 us
    ppermute x2, waiting for transfers between devices, on_device(): theirs = lax.ppermute(grown, 'row', [(d, d ^ reach) for d in range(ways)])  28.3 us
    all_gather x1, waiting for transfers between devices, on_device(): lax.all_gather((mm(m, square) * s).astype(BF), 'row', axis=0, tiled=True)  19.8 us
    all_gather x1, waiting for transfers between devices, on_device(): lax.all_gather(mm(m, pick_col).astype(BF), 'row', axis=0, tiled=True)  15.1 us
    unnamed x7, local copies, waits for them, and re-layouts  8.62 us
    psum x1, blocking collectives, on_device(): total = lax.psum(jnp.sum(m.astype(F32) ** 2), 'row')  6.36 us
    all_gather x1, waiting for transfers between devices, on_device(): panel = lax.all_gather(hamiltonian, 'col', axis=1, tiled=True)  5.01 us
  transfers between devices with their start and end apart: 5, of which 5 were waited for; matrix products, arithmetic and copies ran while one was open for 3% of the time, Pallas kernels for 0%

profile of v1, /device:TPU:0, one launch (start us, length us, event | category | flops | bytes accessed | tf_op | source)
XLA Modules:
  0.0 217.2 jit_solution(16030433524473064689)
XLA Ops:
  6.5 0.0 all-gather.11.cloned.1.call-start
  6.5 0.7 all-gather.11.cloned.1.call-update
  7.3 0.0 all-gather.7.cloned.1.call-start
  7.3 0.7 convert_bitcast_fusion
  8.0 75.1 %all-gather.2 = bf16[32,56,28]{1,2,0:T(8,128)(2,1)S(1)} all-gather(bf16[1,56,28]{1,2,0:T(8,128)(2,1)S(1)} %convert_bitcast_fusion), channel_id=2, replica_groups=mesh['row'=4,'col'=8] {'row','col'}, dimensions={0}, use_global_device_ids=true | all-gather | bytes 103488 | tf_op jit(solution)/shard_map/all_gather | solution.py:29
  83.2 0.2 copy.12
  83.3 0.2 reshape.30
  83.5 0.8 iota_subtract_fusion
  84.3 0.1 select_reduce_fusion.1
  84.4 0.9 convolution_convert_fusion.5
  85.3 0.9 convolution_convert_fusion.4
  86.2 5.0 %all-gather.11.cloned.1.call-done = bf16[8,364,728]{1,2,0:T(8,128)(2,1)} async-done(((bf16[1,364,728]{1,2,0:T(8,128)(2,1)}), bf16[8,364,728]{1,2,0:T(8,128)(2,1)}) %all-gather.11.cloned.1.call-update) | async-done | bytes 4239888 | tf_op jit(solution)/shard_map/all_gather | solution.py:28
  91.2 4.9 %copy.9 = bf16[8,364,728]{1,0,2:T(8,128)(2,1)} copy(bf16[8,364,728]{1,2,0:T(8,128)(2,1)} %all-gather.11.cloned.1.call-done) | data formatting | bytes 8479744 | tf_op jit(solution)/shard_map/all_gather | solution.py:28
  96.1 8.6 %reshape.34 = bf16[2912,728]{0,1:T(8,128)(2,1)} reshape(bf16[8,364,728]{1,0,2:T(8,128)(2,1)} %copy.9) | data formatting | bytes 8479744
  104.7 6.9 %multiply_reduce_fusion = (f32[]{:T(128)}, bf16[728,2912]{1,0:T(8,128)(2,1)}) fusion(s32[224]{0:T(256)S(1)} %get-tuple-element.8, s32[224]{0:T(256)S(1)} %get-tuple-element.7, bf16[56,224]{1,0:T(8,128)(2,1)S(1)} %convolution_convert_fusion.4, s32[56]{0:T(128)S(1)} %get-tuple-element.10, s32[56]{0:T(128)S(1)} %get-tuple-element.9, bf16[2912,728]{0,1:T(8,128)(2,1)} %reshape.34), kind=kOutput, calls=%fused_computation | convolution fusion | flops 987197120 | bytes 8507076 | tf_op jit(solution)/shard_map/dot_general | solution.py:12
  111.5 5.5 %fusion.27 = bf16[728,364]{1,0:T(8,128)(2,1)} fusion(bf16[728,2912]{1,0:T(8,128)(2,1)} %get-tuple-element.6, s32[364]{0:T(512)S(1)} %iota_add_fusion.1), kind=kOutput, calls=%fused_computation.36 | convolution fusion | flops 1544638336 | bytes 4771312 | tf_op jit(solution)/shard_map/dot_general | solution.py:12
  117.1 0.0 all-gather.7.cloned.1.call-update
  117.1 0.0 all-gather.9.cloned.1.call-start
  117.1 6.4 %psum.7 = f32[]{:T(128)} all-reduce(f32[]{:T(128)} %get-tuple-element.5), channel_id=1, replica_groups=mesh['row'=4,'col'=8] {'row'}, use_global_device_ids=true, to_apply=%region_3.4 | all-reduce | flops 1 | bytes 8 | tf_op jit(solution)/shard_map/psum | solution.py:44
  124.2 15.1 %all-gather.7.cloned.1.call-done = bf16[2912,364]{1,0:T(8,128)(2,1)} async-done(((bf16[728,364]{1,0:T(8,128)(2,1)}), bf16[2912,364]{1,0:T(8,128)(2,1)}) %all-gather.7.cloned.1.call-update) | async-done | bytes 2119952 | tf_op jit(solution)/shard_map/all_gather | solution.py:57
  139.3 5.4 %convolution_multiply_fusion = f32[728,364]{1,0:T(8,128)S(1)} fusion(bf16[728,2912]{1,0:T(8,128)(2,1)} %get-tuple-element.6, bf16[2912,364]{1,0:T(8,128)(2,1)} %all-gather.7.cloned.1.call-done, f32[]{:T(128)S(6)} %mul.104), kind=kOutput, calls=%fused_computation.24 | convolution fusion | flops 1543578368 | bytes 7419780 | tf_op jit(solution)/shard_map/dot_general | solution.py:12
  144.7 0.7 fusion.26
  145.4 0.3 collective-permute-start
  145.7 1.7 collective-permute-done
  147.4 0.5 maximum_select_fusion.6
  147.9 0.4 collective-permute-start.1
  148.3 0.0 copy-start.1
  148.3 0.0 copy-start.2
  148.3 26.5 %collective-permute-done.1 = bf16[1456,364]{1,0:T(8,128)(2,1)} collective-permute-done((bf16[1456,364]{1,0:T(8,128)(2,1)S(1)}, bf16[1456,364]{1,0:T(8,128)(2,1)}, u32[]{:S(2)}, u32[]{:S(2)}) %collective-permute-start.1) | collective-permute-done | bytes 1060000 | tf_op jit(solution)/shard_map/ppermute | solution.py:65
  174.8 6.3 %fusion.22 = bf16[728,364]{1,0:T(8,128)(2,1)} fusion(bf16[728,2912]{1,0:T(8,128)(2,1)} %get-tuple-element.6, bf16[1456,364]{1,0:T(8,128)(2,1)} %collective-permute-done.1, bf16[1456,364]{1,0:T(8,128)(2,1)S(1)} %maximum_select_fusion.6, pred[]{:T(512)S(6)} %eq.70, f32[]{:T(128)S(6)} %rsqrt.3), kind=kOutput, calls=%fused_computation.31 | convolution fusion | flops 1553383040 | bytes 6889797 | tf_op jit(solution)/shard_map/dot_general | solution.py:12
  181.1 0.0 all-gather.9.cloned.1.call-update
  181.1 0.0 copy-done.1
  181.1 0.1 iota_subtract_fusion.1
  181.2 0.1 select_reduce_fusion
  181.3 0.0 copy-done.2
  181.4 3.5 %fusion.25 = f32[728,364]{1,0:T(8,128)} fusion(bf16[2912,364]{1,0:T(8,128)(2,1)S(1)} %copy-done.2, s32[728]{0:T(1024)S(1)} %iota_add_fusion, f32[]{:T(128)S(6)} %rsqrt.3), kind=kOutput, calls=%fused_computation.34 | convolution fusion | flops 1546493184 | bytes 3182820 | tf_op jit(solution)/shard_map/dot_general | solution.py:12
  184.9 0.0 copy-start
  184.9 19.8 %all-gather.9.cloned.1.call-done = bf16[2912,364]{1,0:T(8,128)(2,1)} async-done(((bf16[728,364]{1,0:T(8,128)(2,1)}), bf16[2912,364]{1,0:T(8,128)(2,1)}) %all-gather.9.cloned.1.call-update) | async-done | bytes 2119952 | tf_op jit(solution)/shard_map/all_gather | solution.py:71
  204.6 4.4 %fusion.21 = f32[728,364]{1,0:T(8,128)S(1)} fusion(f32[728,364]{1,0:T(8,128)} %fusion.25, bf16[2912,364]{1,0:T(8,128)(2,1)} %all-gather.9.cloned.1.call-done, s32[728]{0:T(1024)S(1)} %iota_add_fusion), kind=kOutput, calls=%fused_computation.30 | convolution fusion | flops 1545963264 | bytes 4242784 | tf_op jit(solution)/shard_map/dot_general | solution.py:12
  209.1 0.0 copy-done
  209.1 1.6 convolution_multiply_fusion.2
  (6 shorter events, 0.0 us)
Async XLA Ops:
  6.5 84.7 %all-gather.11.cloned.1.call-start = ((), (), s32[]{:S(2)}) async-start(), calls=%async_computation.2 | async-start | bytes 5031936 | tf_op jit(solution)/shard_map/all_gather | solution.py:28
  7.3 132.0 %all-gather.7.cloned.1.call-start = ((), (), s32[]{:S(2)}) async-start(), calls=%async_computation | async-start | bytes 2795520 | tf_op jit(solution)/shard_map/all_gather | solution.py:57
  117.1 87.5 %all-gather.9.cloned.1.call-start = ((), (), s32[]{:S(2)}) async-start(), calls=%async_computation.1 | async-start | bytes 2795520 | tf_op jit(solution)/shard_map/all_gather | solution.py:71
  145.4 2.0 collective-permute-start
  147.9 27.0 %collective-permute-start.1 = (bf16[1456,364]{1,0:T(8,128)(2,1)S(1)}, bf16[1456,364]{1,0:T(8,128)(2,1)}, u32[]{:S(2)}, u32[]{:S(2)}) collective-permute-start(bf16[1456,364]{1,0:T(8,128)(2,1)S(1)} %maximum_select_fusion.6), channel_id=1, source_target_pairs={{0,16},{8,24},{16,0},{24,8},{1,17},{9,25},{17,1},{25,9},{2,18},{10... | collective-permute-start | bytes 3179912 | tf_op jit(solution)/shard_map/ppermute | solution.py:65
  148.3 32.9 %copy-start.1 = (s32[224]{0:T(256)S(1)}, s32[224]{0:T(256)}, u32[]{:S(2)}) copy-start(s32[224]{0:T(256)} %param.4) | copy-start | bytes 2692
  148.3 33.1 %copy-start.2 = (bf16[2912,364]{1,0:T(8,128)(2,1)S(1)}, bf16[2912,364]{1,0:T(8,128)(2,1)}, u32[]{:S(2)}) copy-start(bf16[2912,364]{1,0:T(8,128)(2,1)} %all-gather.7.cloned.1.call-done) | copy-start | bytes 6359812
  184.9 24.2 %copy-start = (s32[56,28]{0,1:T(8,128)S(1)}, s32[56,28]{0,1:T(8,128)}, u32[]{:S(2)}) copy-start(s32[56,28]{0,1:T(8,128)} %param.5) | copy-start | bytes 18820
Sparse Core Ops, SparseCore 0:
  9.5 81.6 all-gather.10
  117.2 22.0 all-gather.6
  181.3 23.3 all-gather.8
